TPU v7x, 256 devices: a whole 4x4x8 slice. The times are simulated.
256 devices in a mesh: blk: 128 (over y, x_lo, z, core), rep: 2 (over x_hi).
Axes of the slice: x: 4 (x_hi: 2, x_lo: 2; x = x_hi * 2 + x_lo), y: 4, z: 8, core: 2. Of those that a mesh axis runs over, the one named last changes fastest.
Arguments:
- queries: bfloat16 [32768, 1024], P('blk'), may hold values from -20 to 20
- corpus: bfloat16 [2, 262144, 1024], P('rep', 'blk'), may hold values from -5 to 5
- attributions: bfloat16 [2, 262144, 1024], P('rep', 'blk'), may hold values from -6 to 6
Outputs:
- attributed: bfloat16 [32768, 1024], P('blk')
- log_total: float32 [32768], P('blk')
All inputs are finite; a program needn't handle non-finite values.
Results may differ from a plain program's by a relative error of at most 0.003.
Values may be sent and summed in bfloat16 or wider, within the bound.
A program may use at most 64 MiB of HBM per device.

v0:
```python
import jax
import jax.numpy as jnp
from jax import lax
from jax.sharding import PartitionSpec as P

STEPS = 4


sharpness = 2.5


def from_behind(value, axis, by):
    devices = lax.axis_size(axis)
    return lax.ppermute(value, axis, [(i, (i + by) % devices) for i in range(devices)])


def from_everyone(value, axis):
    devices = lax.axis_size(axis)
    return lax.all_to_all(
        jnp.broadcast_to(value[None], (devices, *value.shape)), axis, 0, 0, tiled=True
    )


def folded_in_pairs(pieces, combine):
    while len(jax.tree.leaves(pieces)[0]) > 1:
        pieces = jax.vmap(combine)(
            *(jax.tree.map(lambda part: part[side::2], pieces) for side in (0, 1))
        )
    return jax.tree.map(lambda part: part[0], pieces)


def joined_all(value, axis, combine):
    pieces = jax.tree.map(lambda part: from_everyone(part, axis), value)
    return folded_in_pairs(pieces, combine)


def partial_stats(block_queries, slab_keys, slab_values):
    scores = jnp.dot(block_queries, slab_keys.T, preferred_element_type=jnp.float32) * (
        sharpness / jnp.sqrt(jnp.float32(block_queries.shape[1]))
    )
    row_max = jnp.max(scores, axis=1)
    weights = jnp.exp(scores - row_max[:, None])
    row_sum = jnp.sum(weights, axis=1)
    weighted = jnp.dot(
        weights.astype(jnp.bfloat16), slab_values, preferred_element_type=jnp.float32
    )
    return (row_max, row_sum, weighted)


def combine(left_part, right_part):
    joined = jnp.maximum(left_part[0], right_part[0])
    left_factor = jnp.exp(left_part[0] - joined)
    right_factor = jnp.exp(right_part[0] - joined)
    row_sum = left_part[1] * left_factor + right_part[1] * right_factor
    weighted = left_part[2] * left_factor[:, None] + right_part[2] * right_factor[:, None]
    return (joined, row_sum, weighted)


def shards(queries, corpus, attributions):
    slab_keys = corpus[0]
    slab_values = attributions[0]
    running = partial_stats(queries, slab_keys, slab_values)
    visiting = queries
    for rounds in range(STEPS - 1):
        visiting = from_behind(visiting, "blk", 1)
        moved = from_behind((running[0], running[1], running[2]), "blk", 1)
        running = combine(moved, partial_stats(visiting, slab_keys, slab_values))
    running = from_behind((running[0], running[1], running[2]), "blk", 1 - STEPS)
    running = joined_all((running[0], running[1], running[2]), "rep", combine)
    attributed = (running[2] / running[1][:, None]).astype(jnp.bfloat16)
    log_total = running[0] + jnp.log(running[1])
    return (attributed, log_total)


def solution(mesh):
    return jax.shard_map(
        shards,
        mesh=mesh,
        in_specs=(P("blk", None), P("rep", "blk", None), P("rep", "blk", None)),
        out_specs=(P("blk", None), P("blk")),
        check_vma=False,
    )
```

profile of v0, /device:TPU:0, one launch (start us, length us, event | category | flops | bytes accessed | tf_op | source)
XLA Modules:
  0.0 151.5 jit_solution(17339486236163732405)
XLA Ops:
  0.7 3.9 %fusion.53 = (f32[256]{0:T(256)S(1)}, f32[256,2048]{1,0:T(8,128)S(1)}) fusion(bf16[256,1024]{1,0:T(8,128)(2,1)} %param.3, bf16[1,2048,1024]{2,1,0:T(8,128)(2,1)} %param.4), kind=kOutput, calls=%fused_computation.63 | convolution fusion | flops 1074790144 | bytes 6816768 | tf_op jit(solution)/shard_map/dot_general | solution.py:38
  4.6 1.4 fusion.6
  6.0 0.2 collective-permute-start
  6.4 0.4 fusion.28
  6.8 1.9 %collective-permute-start.11 = (f32[256]{0:T(256)S(1)}, f32[256]{0:T(256)S(1)}, u32[]{:S(2)}, u32[]{:S(2)}) collective-permute-start(f32[256]{0:T(256)S(1)} %fusion.28), channel_id=1, source_target_pairs={{0,2},{2,4},{4,6},{6,8},{8,10},{10,12},{12,14},{14,16},{16,18},{18... | collective-permute-start | bytes 3080 | tf_op jit(solution)/shard_map/ppermute | solution.py:14
  8.8 6.0 %collective-permute-done.2 = bf16[256,1024]{1,0:T(8,128)(2,1)S(1)} collective-permute-done((bf16[256,1024]{1,0:T(8,128)(2,1)}, bf16[256,1024]{1,0:T(8,128)(2,1)S(1)}, u32[]{:S(2)}, u32[]{:S(2)}) %collective-permute-start.2) | collective-permute-done | bytes 524320 | tf_op jit(solution)/shard_map/ppermute | solution.py:14
  14.8 1.4 fusion.52
  16.1 0.4 fusion.30
  16.6 9.5 %collective-permute-done.11 = f32[256]{0:T(256)S(1)} collective-permute-done((f32[256]{0:T(256)S(1)}, f32[256]{0:T(256)S(1)}, u32[]{:S(2)}, u32[]{:S(2)}) %collective-permute-start.11) | collective-permute-done | bytes 1056 | tf_op jit(solution)/shard_map/ppermute | solution.py:14
  26.4 1.4 multiply_add_fusion.2
  27.8 0.3 collective-permute-start.3
  28.0 11.1 %collective-permute-done.5 = bf16[256,1024]{1,0:T(8,128)(2,1)S(1)} collective-permute-done((bf16[256,1024]{1,0:T(8,128)(2,1)S(1)}, bf16[256,1024]{1,0:T(8,128)(2,1)S(1)}, u32[]{:S(2)}, u32[]{:S(2)}) %collective-permute-start.5) | collective-permute-done | bytes 524320 | tf_op jit(solution)/shard_map/ppermute | solution.py:14
  39.2 1.4 fusion.51
  40.5 1.4 fusion.2
  41.9 0.4 fusion.32
  42.7 7.7 %collective-permute-done.3 = f32[256,1024]{1,0:T(8,128)S(1)} collective-permute-done((f32[256,1024]{1,0:T(8,128)S(1)}, f32[256,1024]{1,0:T(8,128)S(1)}, u32[]{:S(2)}, u32[]{:S(2)}) %collective-permute-start.3) | collective-permute-done | bytes 1048608 | tf_op jit(solution)/shard_map/ppermute | solution.py:14
  50.7 5.3 %collective-permute-done.8 = bf16[256,1024]{1,0:T(8,128)(2,1)S(1)} collective-permute-done((bf16[256,1024]{1,0:T(8,128)(2,1)S(1)}, bf16[256,1024]{1,0:T(8,128)(2,1)S(1)}, u32[]{:S(2)}, u32[]{:S(2)}) %collective-permute-start.8) | collective-permute-done | bytes 524320 | tf_op jit(solution)/shard_map/ppermute | solution.py:14
  56.0 1.4 fusion.50
  57.4 0.4 fusion.34
  57.9 1.4 fusion
  59.2 9.9 %collective-permute-done.6 = f32[256,1024]{1,0:T(8,128)S(1)} collective-permute-done((f32[256,1024]{1,0:T(8,128)S(1)}, f32[256,1024]{1,0:T(8,128)S(1)}, u32[]{:S(2)}, u32[]{:S(2)}) %collective-permute-start.6) | collective-permute-done | bytes 1048608 | tf_op jit(solution)/shard_map/ppermute | solution.py:14
  69.1 0.2 multiply_add_fusion
  69.6 34.2 %collective-permute-done.14 = f32[256]{0:T(256)S(1)} collective-permute-done((f32[256]{0:T(256)S(1)}, f32[256]{0:T(256)S(1)}, u32[]{:S(2)}, u32[]{:S(2)}) %collective-permute-start.14) | collective-permute-done | bytes 1056 | tf_op jit(solution)/shard_map/ppermute | solution.py:14
  103.8 0.6 broadcast_in_dim.8
  104.4 4.0 %all-to-all-start.2 = ((f32[2,1,256]{2,1,0:T(1,128)}), f32[2,1,256]{2,1,0:T(1,128)S(1)}, u32[]{:S(2)}, u32[]{:S(2)}) async-start(f32[2,1,256]{2,1,0:T(1,128)} %broadcast_in_dim.8), calls=%async_computation.2 | async-start | bytes 4096 | tf_op jit(solution)/shard_map/all_to_all | solution.py:19
  108.4 5.3 %all-to-all-done.2 = f32[2,1,256]{2,1,0:T(1,128)S(1)} async-done(((f32[2,1,256]{2,1,0:T(1,128)}), f32[2,1,256]{2,1,0:T(1,128)S(1)}, u32[]{:S(2)}, u32[]{:S(2)}) %all-to-all-start.2) | async-done | bytes 2080 | tf_op jit(solution)/shard_map/all_to_all | solution.py:19
  113.7 7.6 %all_to_all.17 = f32[2,1,256]{2,1,0:T(1,128)S(1)} all-to-all(f32[2,1,256]{2,1,0:T(1,128)S(1)} %broadcast_in_dim.7), channel_id=1, replica_groups=mesh['blk'=128,'rep'=2] {'rep'}, dimensions={0} | all-to-all | bytes 4096 | tf_op jit(solution)/shard_map/all_to_all | solution.py:19
  121.3 1.6 %broadcast_in_dim.6 = f32[2,256,1024]{2,1,0:T(8,128)} broadcast(f32[256,1024]{1,0:T(8,128)S(1)} %collective-permute-done.9), dimensions={1,2} | broadcast | bytes 3145728 | tf_op jit(solution)/shard_map/broadcast_in_dim | solution.py:20
  122.9 3.8 %all-to-all-start = ((f32[2,256,1024]{2,1,0:T(8,128)}), f32[2,256,1024]{2,1,0:T(8,128)S(1)}, u32[]{:S(2)}, u32[]{:S(2)}) async-start(f32[2,256,1024]{2,1,0:T(8,128)} %broadcast_in_dim.6), calls=%async_computation | async-start | bytes 4194304 | tf_op jit(solution)/shard_map/all_to_all | solution.py:19
  126.7 0.6 log_add_fusion
  127.2 23.2 %all-to-all-done = f32[2,256,1024]{2,1,0:T(8,128)S(1)} async-done(((f32[2,256,1024]{2,1,0:T(8,128)}), f32[2,256,1024]{2,1,0:T(8,128)S(1)}, u32[]{:S(2)}, u32[]{:S(2)}) %all-to-all-start) | async-done | bytes 2097184 | tf_op jit(solution)/shard_map/all_to_all | solution.py:19
  150.4 1.0 fusion.47
  (31 shorter events, 1.3 us)
Async XLA Ops:
  0.6 4.0 %copy-start.1 = (bf16[1,2048,1024]{2,1,0:T(8,128)(2,1)S(1)}, bf16[1,2048,1024]{2,1,0:T(8,128)(2,1)}, u32[]{:S(2)}) copy-start(bf16[1,2048,1024]{2,1,0:T(8,128)(2,1)} %param.5) | copy-start | bytes 12582916
  0.6 14.1 %collective-permute-start.2 = (bf16[256,1024]{1,0:T(8,128)(2,1)}, bf16[256,1024]{1,0:T(8,128)(2,1)S(1)}, u32[]{:S(2)}, u32[]{:S(2)}) collective-permute-start(bf16[256,1024]{1,0:T(8,128)(2,1)} %param.3), channel_id=1, source_target_pairs={{0,2},{2,4},{4,6},{6,8},{8,10},{10,12},{12,14},{14,16},{16,18},{18... | collective-permute-start | bytes 1572872 | tf_op jit(solution)/shard_map/ppermute | solution.py:14
  4.6 10.2 %copy-start = (bf16[1,2048,1024]{2,1,0:T(8,128)(2,1)S(1)}, bf16[1,2048,1024]{2,1,0:T(8,128)(2,1)}, u32[]{:S(2)}) copy-start(bf16[1,2048,1024]{2,1,0:T(8,128)(2,1)} %param.4) | copy-start | bytes 12582916
  6.0 20.4 %collective-permute-start = (f32[256,1024]{1,0:T(8,128)S(1)}, f32[256,1024]{1,0:T(8,128)S(1)}, u32[]{:S(2)}, u32[]{:S(2)}) collective-permute-start(f32[256,1024]{1,0:T(8,128)S(1)} %fusion.6), channel_id=1, source_target_pairs={{0,2},{2,4},{4,6},{6,8},{8,10},{10,12},{12,14},{14,16},{16,18},{18... | collective-permute-start | bytes 3145736 | tf_op jit(solution)/shard_map/ppermute | solution.py:14
  6.2 19.8 %collective-permute-start.1 = (f32[256]{0:T(256)S(1)}, f32[256]{0:T(256)S(1)}, u32[]{:S(2)}, u32[]{:S(2)}) collective-permute-start(f32[256]{0:T(256)S(1)} %get-tuple-element.28), channel_id=1, source_target_pairs={{0,2},{2,4},{4,6},{6,8},{8,10},{10,12},{12,14},{14,16},{16,18},{18... | collective-permute-start | bytes 3080 | tf_op jit(solution)/shard_map/ppermute | solution.py:14
  6.8 19.2 %collective-permute-start.11 = (f32[256]{0:T(256)S(1)}, f32[256]{0:T(256)S(1)}, u32[]{:S(2)}, u32[]{:S(2)}) collective-permute-start(f32[256]{0:T(256)S(1)} %fusion.28), channel_id=1, source_target_pairs={{0,2},{2,4},{4,6},{6,8},{8,10},{10,12},{12,14},{14,16},{16,18},{18... | collective-permute-start | bytes 3080 | tf_op jit(solution)/shard_map/ppermute | solution.py:14
  26.1 16.4 %collective-permute-start.12 = (f32[256]{0:T(256)S(1)}, f32[256]{0:T(256)S(1)}, u32[]{:S(2)}, u32[]{:S(2)}) collective-permute-start(f32[256]{0:T(256)S(1)} %get-tuple-element.14), channel_id=1, source_target_pairs={{0,2},{2,4},{4,6},{6,8},{8,10},{10,12},{12,14},{14,16},{16,18},{18... | collective-permute-start | bytes 3080 | tf_op jit(solution)/shard_map/ppermute | solution.py:14
  26.2 16.3 %collective-permute-start.4 = (f32[256]{0:T(256)S(1)}, f32[256]{0:T(256)S(1)}, u32[]{:S(2)}, u32[]{:S(2)}) collective-permute-start(f32[256]{0:T(256)S(1)} %get-tuple-element.17), channel_id=1, source_target_pairs={{0,2},{2,4},{4,6},{6,8},{8,10},{10,12},{12,14},{14,16},{16,18},{18... | collective-permute-start | bytes 3080 | tf_op jit(solution)/shard_map/ppermute | solution.py:14
  26.3 12.9 %collective-permute-start.5 = (bf16[256,1024]{1,0:T(8,128)(2,1)S(1)}, bf16[256,1024]{1,0:T(8,128)(2,1)S(1)}, u32[]{:S(2)}, u32[]{:S(2)}) collective-permute-start(bf16[256,1024]{1,0:T(8,128)(2,1)S(1)} %collective-permute-done.2), channel_id=1, source_target_pairs={{0,2},{2,4},{4,6},{6,8},{8,10},{10,12},{12,14},{14,16},{16,18},{18... | collective-permute-start | bytes 1572872 | tf_op jit(solution)/shard_map/ppermute | solution.py:14
  27.8 22.6 %collective-permute-start.3 = (f32[256,1024]{1,0:T(8,128)S(1)}, f32[256,1024]{1,0:T(8,128)S(1)}, u32[]{:S(2)}, u32[]{:S(2)}) collective-permute-start(f32[256,1024]{1,0:T(8,128)S(1)} %multiply_add_fusion.2), channel_id=1, source_target_pairs={{0,2},{2,4},{4,6},{6,8},{8,10},{10,12},{12,14},{14,16},{16,18},{18... | collective-permute-start | bytes 3145736 | tf_op jit(solution)/shard_map/ppermute | solution.py:14
  42.4 13.7 %collective-permute-start.8 = (bf16[256,1024]{1,0:T(8,128)(2,1)S(1)}, bf16[256,1024]{1,0:T(8,128)(2,1)S(1)}, u32[]{:S(2)}, u32[]{:S(2)}) collective-permute-start(bf16[256,1024]{1,0:T(8,128)(2,1)S(1)} %collective-permute-done.5), channel_id=1, source_target_pairs={{0,2},{2,4},{4,6},{6,8},{8,10},{10,12},{12,14},{14,16},{16,18},{18... | collective-permute-start | bytes 1572872 | tf_op jit(solution)/shard_map/ppermute | solution.py:14
  42.5 15.3 %collective-permute-start.13 = (f32[256]{0:T(256)S(1)}, f32[256]{0:T(256)S(1)}, u32[]{:S(2)}, u32[]{:S(2)}) collective-permute-start(f32[256]{0:T(256)S(1)} %get-tuple-element.10), channel_id=1, source_target_pairs={{0,2},{2,4},{4,6},{6,8},{8,10},{10,12},{12,14},{14,16},{16,18},{18... | collective-permute-start | bytes 3080 | tf_op jit(solution)/shard_map/ppermute | solution.py:14
  42.6 15.3 %collective-permute-start.7 = (f32[256]{0:T(256)S(1)}, f32[256]{0:T(256)S(1)}, u32[]{:S(2)}, u32[]{:S(2)}) collective-permute-start(f32[256]{0:T(256)S(1)} %get-tuple-element.13), channel_id=1, source_target_pairs={{0,2},{2,4},{4,6},{6,8},{8,10},{10,12},{12,14},{14,16},{16,18},{18... | collective-permute-start | bytes 3080 | tf_op jit(solution)/shard_map/ppermute | solution.py:14
  50.6 18.5 %collective-permute-start.6 = (f32[256,1024]{1,0:T(8,128)S(1)}, f32[256,1024]{1,0:T(8,128)S(1)}, u32[]{:S(2)}, u32[]{:S(2)}) collective-permute-start(f32[256,1024]{1,0:T(8,128)S(1)} %multiply_add_fusion.1), channel_id=1, source_target_pairs={{0,2},{2,4},{4,6},{6,8},{8,10},{10,12},{12,14},{14,16},{16,18},{18... | collective-permute-start | bytes 3145736 | tf_op jit(solution)/shard_map/ppermute | solution.py:14
  69.3 51.9 %collective-permute-start.9 = (f32[256,1024]{1,0:T(8,128)S(1)}, f32[256,1024]{1,0:T(8,128)S(1)}, u32[]{:S(2)}, u32[]{:S(2)}) collective-permute-start(f32[256,1024]{1,0:T(8,128)S(1)} %multiply_add_fusion), channel_id=1, source_target_pairs={{0,250},{2,252},{4,254},{6,0},{8,2},{10,4},{12,6},{14,8},{16,10},{... | collective-permute-start | bytes 3145736 | tf_op jit(solution)/shard_map/ppermute | solution.py:14
  69.4 34.4 %collective-permute-start.14 = (f32[256]{0:T(256)S(1)}, f32[256]{0:T(256)S(1)}, u32[]{:S(2)}, u32[]{:S(2)}) collective-permute-start(f32[256]{0:T(256)S(1)} %get-tuple-element.6), channel_id=1, source_target_pairs={{0,250},{2,252},{4,254},{6,0},{8,2},{10,4},{12,6},{14,8},{16,10},{... | collective-permute-start | bytes 3080 | tf_op jit(solution)/shard_map/ppermute | solution.py:14
  69.5 38.9 %collective-permute-start.10 = (f32[256]{0:T(256)S(1)}, f32[256]{0:T(256)S(1)}, u32[]{:S(2)}, u32[]{:S(2)}) collective-permute-start(f32[256]{0:T(256)S(1)} %get-tuple-element.9), channel_id=1, source_target_pairs={{0,250},{2,252},{4,254},{6,0},{8,2},{10,4},{12,6},{14,8},{16,10},{... | collective-permute-start | bytes 3080 | tf_op jit(solution)/shard_map/ppermute | solution.py:14
  104.4 9.3 %all-to-all-start.2 = ((f32[2,1,256]{2,1,0:T(1,128)}), f32[2,1,256]{2,1,0:T(1,128)S(1)}, u32[]{:S(2)}, u32[]{:S(2)}) async-start(f32[2,1,256]{2,1,0:T(1,128)} %broadcast_in_dim.8), calls=%async_computation.2 | async-start | bytes 4096 | tf_op jit(solution)/shard_map/all_to_all | solution.py:19
  122.9 27.6 %all-to-all-start = ((f32[2,256,1024]{2,1,0:T(8,128)}), f32[2,256,1024]{2,1,0:T(8,128)S(1)}, u32[]{:S(2)}, u32[]{:S(2)}) async-start(f32[2,256,1024]{2,1,0:T(8,128)} %broadcast_in_dim.6), calls=%async_computation | async-start | bytes 4194304 | tf_op jit(solution)/shard_map/all_to_all | solution.py:19
where the time goes:
time: 152 us; the launch traced here: 151 us
  waiting for transfers between devices  112 us (74%)
  matrix products  13.5 us (9%)
  starting transfers between devices  11.3 us (7%)
  blocking collectives  7.6 us (5%)
  other arithmetic  3.76 us (2%)
  local copies, waits for them, and re-layouts  2.2 us (1%)
    ppermute x15, waiting for transfers between devices, from_behind(): lax.ppermute(value, axis, [(i, (i + by) % devices) for i in range(devices)])  83.7 us
    all_to_all x2, waiting for transfers between devices, from_everyone(): lax.all_to_all(jnp.broadcast_to(value[None], (devices, *value.shape)), ax...  28.5 us
    dot_general x4, matrix products, partial_stats(): jnp.dot(block_queries, slab_keys.T, preferred_element_type=jnp.float32)  7.99 us
    all_to_all x2, starting transfers between devices, from_everyone(): lax.all_to_all(jnp.broadcast_to(value[None], (devices, *value.shape)), ax...  7.76 us
    all_to_all x1, blocking collectives, from_everyone(): lax.all_to_all(jnp.broadcast_to(value[None], (devices, *value.shape)), ax...  7.6 us
    dot_general x4, matrix products, partial_stats(): jnp.dot(weights.astype(jnp.bfloat16), slab_values, preferred_element_type...  5.53 us
    ppermute x15, starting transfers between devices, from_behind(): lax.ppermute(value, axis, [(i, (i + by) % devices) for i in range(devices)])  3.53 us
  transfers between devices with their start and end apart: 17, of which 9 were waited for; matrix products, arithmetic and copies ran while one was open for 11% of the time, Pallas kernels for 0%

commit v1 on v0

v1 whole, which is shorter than its diff:
```python
import functools
import math

import jax
import jax.numpy as jnp
from jax import lax
from jax.experimental import pallas as pl
from jax.experimental.pallas import tpu as pltpu
from jax.sharding import PartitionSpec as P

MESH = pl.DeviceIdType.MESH
SHARPNESS = 2.5
PARTS = 2
TO_NEXT_CHIP, TO_NEXT, TO_CORE, SIDE, SIDE_L, BACK, BACK_L, OWN, OWN_L, HOME, HOME_L, HOME2, HOME2_L, FINAL = range(14)
NEVER = -1e30


def as_column(tile, rows):
    return jnp.broadcast_to(tile[0:1], (128, rows)).T[:, 0:1]


def as_tile(column, rows):
    return jnp.broadcast_to(column, (rows, 128)).T[0:8]


def log_sum(terms):
    top = functools.reduce(jnp.maximum, terms)
    return top + jnp.log(sum(jnp.exp(t - top) for t in terms))


def kernel(
    n, q_hbm, k_hbm, v_hbm, out_hbm, log_ref,
    qs, ks, vs, pf, r1, p3, r3, xs, rx, ms, rm, own, fin, lp, l1, l3, lo, lx, lm, lr,
    load_sem, send_sem, recv_sem, out_sem,
):
    b = lax.axis_index("blk")
    r = lax.axis_index("rep")
    c = lax.rem(b, 2)
    block, depth = q_hbm.shape
    half = vs.shape[1] // 2
    rows = block // PARTS

    def at(step, rep=None):
        return (lax.rem(b + n + step, n), r if rep is None else rep)

    partner = at(1 - 2 * c)

    def part(g):
        return pl.ds(g * rows, rows)

    def remote(kind, g, src, dst, device, land=None):
        return pltpu.make_async_remote_copy(
            src_ref=src, dst_ref=dst,
            send_sem=send_sem.at[kind, g],
            recv_sem=recv_sem.at[kind if land is None else land, g],
            device_id=device, device_id_type=MESH,
        )

    loads = [pltpu.make_async_copy(q_hbm, qs.at[0], load_sem.at[0]),
             pltpu.make_async_copy(k_hbm.at[0], ks, load_sem.at[1]),
             pltpu.make_async_copy(v_hbm.at[0], vs, load_sem.at[2])]
    for load in loads:
        load.start()

    barrier = pltpu.get_barrier_semaphore()
    for device in (at(-2), at(-1), at(1), at(2), at(2, 1 - r), at(0, 1 - r)):
        pl.semaphore_signal(barrier, inc=1, device_id=device, device_id_type=MESH)
    pl.semaphore_wait(barrier, 6)

    def next_chip(g):
        return remote(TO_NEXT_CHIP, g, qs.at[0, part(g)], qs.at[2, part(g)], at(2))

    def next_block(g):
        return remote(TO_NEXT, g, qs.at[2, part(g)], qs.at[3, part(g)], at(1))

    def next_core(g):
        return remote(TO_CORE, g, qs.at[2 * c, part(g)], qs.at[1, part(g)], partner)

    def side(g):
        return (remote(SIDE, g, pf.at[1, :, part(g)], r1.at[:, part(g)], partner),
                remote(SIDE_L, g, lp.at[1, g], l1.at[g], partner))

    def back(g):
        return (remote(BACK, g, p3.at[:, part(g)], r3.at[:, part(g)], at(-1)),
                remote(BACK_L, g, lp.at[3, g], l3.at[g], at(-1)))

    def across(g):
        return (remote(OWN, g, xs.at[part(g)], rx.at[part(g)], at(0, 1 - r)),
                remote(OWN_L, g, lo.at[g], lx.at[g], at(0, 1 - r)))

    def home(g, j, source):
        return (remote(HOME + 2 * j, g, ms.at[j, part(g)], rm.at[source, part(g)], at(-2, j), HOME + 2 * source),
                remote(HOME_L + 2 * j, g, lm.at[g], lr.at[source, g], at(-2, j), HOME_L + 2 * source))

    def final(g, column):
        return remote(FINAL, g, fin.at[part(g)], out_hbm.at[part(g), column], at(0, 1 - r))

    def start(*copies):
        for copy in copies:
            copy.start()

    def arrived(*copies):
        for copy in copies:
            copy.wait_recv()

    scale = SHARPNESS / math.sqrt(depth)

    def attend(slot, g):
        d = lax.dot_general(qs[slot, part(g)], ks[...], (((1,), (1,)), ((), ())), preferred_element_type=jnp.float32)
        top = jnp.max(d, axis=1, keepdims=True)
        weights = jnp.exp2((d - top) * (scale * math.log2(math.e)))
        total = jnp.sum(weights, axis=1, keepdims=True)
        low = weights.astype(jnp.bfloat16)
        share = 1.0 / total
        for j in range(2):
            pf[slot, j, part(g)] = share * jnp.dot(low, vs[:, j * half:(j + 1) * half], preferred_element_type=jnp.float32)
        lp[slot, g] = as_tile(top * scale + jnp.log(total), rows)

    loads[0].wait()

    @pl.when(c == 0)
    def _():
        for g in range(PARTS):
            next_core(g).start()

    for g in range(PARTS):
        next_chip(g).start()
    loads[1].wait()
    loads[2].wait()
    for g in range(PARTS):
        attend(0, g)

    for g in range(PARTS):
        @pl.when(c == 1)
        def _():
            arrived(next_chip(g))
            start(next_block(g), next_core(g))
        arrived(next_core(g))
        attend(1, g)
        start(*side(g))

    def returned(g):
        p3[:, part(g)] = pf[3, :, part(g)].astype(jnp.bfloat16)
        start(*back(g))

    for g in range(PARTS):
        @pl.when(c == 0)
        def _():
            arrived(next_chip(g))
            start(next_block(g))
            arrived(next_block(g))
        attend(3 - c, g)

        @pl.when(c == 0)
        def _():
            returned(g)

    for g in range(PARTS):
        arrived(*side(g))
        ours = as_column(lp[0, g], rows)
        theirs = jnp.where(c == 0, as_column(l1[g], rows), NEVER)
        both = log_sum([ours, theirs])
        ours, theirs = jnp.exp(ours - both), jnp.exp(theirs - both)
        xs[part(g)] = (ours * pf[0, 1 - r, part(g)] + theirs * r1[1 - r, part(g)]).astype(jnp.bfloat16)
        own[part(g)] = ours * pf[0, r, part(g)] + theirs * r1[r, part(g)]
        lo[g] = as_tile(both, rows)
        start(*across(g))

    for g in range(PARTS):
        @pl.when(c == 1)
        def _():
            arrived(next_block(g))
        attend(2 + c, g)

        @pl.when(c == 1)
        def _():
            returned(g)
        arrived(*back(g))
        mine = as_column(lp[2, g], rows)
        core = jnp.where(c == 1, as_column(l1[g], rows), NEVER)
        behind = as_column(l3[g], rows)
        both = log_sum([mine, core, behind])
        mine, core, behind = jnp.exp(mine - both), jnp.exp(core - both), jnp.exp(behind - both)
        lm[g] = as_tile(both, rows)
        for j in range(2):
            ms[j, part(g)] = (mine * pf[2, j, part(g)] + core * r1[j, part(g)]
                              + behind * r3[j, part(g)].astype(jnp.float32)).astype(jnp.bfloat16)
            start(*home(g, j, r))

    column = pl.ds(pl.multiple_of(r * half, half), half)
    outs = []
    for g in range(PARTS):
        arrived(*across(g), *home(g, 0, 0), *home(g, 1, 1))
        logs = [as_column(t, rows) for t in (lo[g], lx[g], lr[0, g], lr[1, g])]
        both = log_sum(logs)
        w = [jnp.exp(t - both) for t in logs]
        fin[part(g)] = (w[0] * own[part(g)] + w[1] * rx[part(g)].astype(jnp.float32)
                        + w[2] * rm[0, part(g)].astype(jnp.float32)
                        + w[3] * rm[1, part(g)].astype(jnp.float32)).astype(jnp.bfloat16)
        final(g, column).start()
        out = pltpu.make_async_copy(fin.at[part(g)], out_hbm.at[part(g), column], out_sem.at[g])
        out.start()
        outs.append(out)
        log_ref[g:g + 1] = as_tile(both, rows)[0:1]

    for out in outs:
        out.wait()
    for g in range(PARTS):
        arrived(final(g, column))
        for copy in (next_chip(g), next_block(g), next_core(g), *side(g), *back(g), *across(g),
                     *home(g, 0, r), *home(g, 1, r), final(g, column)):
            copy.wait_send()


def shards(n, queries, corpus, attributions):
    block, depth = queries.shape
    slab, width = attributions.shape[1:]
    rows, half = block // PARTS, width // 2
    low, full = jnp.bfloat16, jnp.float32
    hbm = pl.BlockSpec(memory_space=pl.ANY)
    attributed, log_total = pl.pallas_call(
        functools.partial(kernel, n),
        out_shape=(jax.ShapeDtypeStruct((block, width), low), jax.ShapeDtypeStruct((PARTS, rows), full)),
        in_specs=[hbm] * 3,
        out_specs=(hbm, pl.BlockSpec(memory_space=pltpu.VMEM)),
        scratch_shapes=[
            pltpu.VMEM((4, block, depth), low),
            pltpu.VMEM((slab, depth), low),
            pltpu.VMEM((slab, width), low),
            pltpu.VMEM((4, 2, block, half), full),
            pltpu.VMEM((2, block, half), full),
            pltpu.VMEM((2, block, half), low),
            pltpu.VMEM((2, block, half), low),
            pltpu.VMEM((block, half), low),
            pltpu.VMEM((block, half), low),
            pltpu.VMEM((2, block, half), low),
            pltpu.VMEM((2, block, half), low),
            pltpu.VMEM((block, half), full),
            pltpu.VMEM((block, half), low),
            pltpu.VMEM((4, PARTS, 8, rows), full),
            pltpu.VMEM((PARTS, 8, rows), full),
            pltpu.VMEM((PARTS, 8, rows), full),
            pltpu.VMEM((PARTS, 8, rows), full),
            pltpu.VMEM((PARTS, 8, rows), full),
            pltpu.VMEM((PARTS, 8, rows), full),
            pltpu.VMEM((2, PARTS, 8, rows), full),
            pltpu.SemaphoreType.DMA((3,)),
            pltpu.SemaphoreType.DMA((14, PARTS)),
            pltpu.SemaphoreType.DMA((14, PARTS)),
            pltpu.SemaphoreType.DMA((PARTS,)),
        ],
        compiler_params=pltpu.CompilerParams(collective_id=0, has_side_effects=True, vmem_limit_bytes=60 << 20),
    )(queries, corpus, attributions)
    return attributed, log_total.reshape(block)


def solution(mesh):
    return jax.shard_map(
        functools.partial(shards, mesh.shape["blk"]),
        mesh=mesh,
        in_specs=(P("blk", None), P("rep", "blk", None), P("rep", "blk", None)),
        out_specs=(P("blk", None), P("blk")),
        check_vma=False,
    )
```

time: 152 us -> 58.4 us (0.38)
  waiting for transfers between devices: 112 us -> 0 us
  Pallas kernels: 0 us -> 54.2 us
  matrix products: 13.5 us -> 0 us
  starting transfers between devices: 11.3 us -> 0 us
  blocking collectives: 7.6 us -> 0 us
  other arithmetic: 3.76 us -> 0 us
    ppermute x15 -> x0, waiting for transfers between devices: 83.7 us -> none  [from_behind(): lax.ppermute(value, axis, [(i, (i + by) % devices) for i in range(devices)])]
    pallas_call x0 -> x1, Pallas kernels: none -> 54.2 us  [shards(): pl.pallas_call(functools.partial(kernel, n), out_shape=(jax.ShapeDtypeStr...]
    all_to_all x2 -> x0, waiting for transfers between devices: 28.5 us -> none  [from_everyone(): lax.all_to_all(jnp.broadcast_to(value[None], (devices, *value.shape)), ax...]
    dot_general x8 -> x0, matrix products: 13.5 us -> none  [the longest x4 7.99 us: partial_stats(): jnp.dot(block_queries, slab_keys.T, preferred_element_type=jnp.float32)]
    all_to_all x2 -> x0, starting transfers between devices: 7.76 us -> none  [from_everyone(): lax.all_to_all(jnp.broadcast_to(value[None], (devices, *value.shape)), ax...]
    all_to_all x1 -> x0, blocking collectives: 7.6 us -> none  [from_everyone(): lax.all_to_all(jnp.broadcast_to(value[None], (devices, *value.shape)), ax...]
    ppermute x15 -> x0, starting transfers between devices: 3.53 us -> none  [from_behind(): lax.ppermute(value, axis, [(i, (i + by) % devices) for i in range(devices)])]
    unnamed x4 -> x2, local copies, waits for them, and re-layouts: 0.01 us -> 3.07 us
  transfers between devices with their start and end apart: 17 -> 0, of which waited for: 9 -> 0; matrix products, arithmetic and copies ran while one was open for 11% -> 0% of each run, Pallas kernels for 0% -> 0%
where the time goes in v1:
time: 58.4 us; the launch traced here: 57.9 us
  Pallas kernels  54.2 us (93%)
  local copies, waits for them, and re-layouts  3.07 us (5%)
  between operations  0.64 us (1%)
    pallas_call x1, Pallas kernels, shards(): pl.pallas_call(functools.partial(kernel, n), out_shape=(jax.ShapeDtypeStr...  54.2 us
    unnamed x2, local copies, waits for them, and re-layouts  3.07 us

profile of v1, /device:TPU:0, one launch (start us, length us, event | category | flops | bytes accessed | tf_op | source)
XLA Modules:
  0.0 57.9 jit_solution(9832101150990077335)
XLA Ops:
  0.6 54.2 %shard_map.50 = (bf16[256,1024]{1,0:T(8,128)(2,1)}, f32[2,128]{1,0:T(2,128)}) custom-call(bf16[256,1024]{1,0:T(8,128)(2,1)} %q_hbm.1, bf16[1,2048,1024]{2,1,0:T(8,128)(2,1)} %k_hbm.1, bf16[1,2048,1024]{2,1,0:T(8,128)(2,1)} %v_hbm.1), custom_call_target="tpu_custom_call" | custom-call | tf_op jit(solution)/shard_map/pallas_call | solution.py:221
  54.9 1.9 %copy.7 = bf16[256,1024]{1,0:T(8,128)(2,1)} copy(bf16[256,1024]{1,0:T(8,128)(2,1)} %get-tuple-element.8) | data formatting | bytes 1048576
  56.7 1.2 %copy.8 = f32[256]{0:T(256)} copy(f32[256]{0:T(256)} %bitcast.1) | data formatting | bytes 2048

commit v2 on v1

--- a/solution.py
+++ b/solution.py
@@ -11,8 +11,10 @@
 MESH = pl.DeviceIdType.MESH
 SHARPNESS = 2.5
 PARTS = 2
+CHUNKS = 4
 TO_NEXT_CHIP, TO_NEXT, TO_CORE, SIDE, SIDE_L, BACK, BACK_L, OWN, OWN_L, HOME, HOME_L, HOME2, HOME2_L, FINAL = range(14)
 NEVER = -1e30
+RING = 8
 
 
 def as_column(tile, rows):
@@ -30,15 +32,18 @@
 
 def kernel(
     n, q_hbm, k_hbm, v_hbm, out_hbm, log_ref,
-    qs, ks, vs, pf, r1, p3, r3, xs, rx, ms, rm, own, fin, lp, l1, l3, lo, lx, lm, lr,
-    load_sem, send_sem, recv_sem, out_sem,
+    qs, ks, kt, vs, pf, r1, p3, r3, xs, rx, ms, rm, own, fin, lp, l1, l3, lo, lx, lm, lr,
+    load_sem, send_sem, recv_sem, out_sem, ready,
 ):
     b = lax.axis_index("blk")
     r = lax.axis_index("rep")
     c = lax.rem(b, 2)
+    place = lax.rem(b // 2, RING)
     block, depth = q_hbm.shape
     half = vs.shape[1] // 2
     rows = block // PARTS
+    few = block // CHUNKS
+    each = CHUNKS // PARTS
 
     def at(step, rep=None):
         return (lax.rem(b + n + step, n), r if rep is None else rep)
@@ -47,6 +52,9 @@
 
     def part(g):
         return pl.ds(g * rows, rows)
+
+    def chunk(i):
+        return pl.ds(i * few, few)
 
     def remote(kind, g, src, dst, device, land=None):
         return pltpu.make_async_remote_copy(
@@ -63,18 +71,27 @@
         load.start()
 
     barrier = pltpu.get_barrier_semaphore()
-    for device in (at(-2), at(-1), at(1), at(2), at(2, 1 - r), at(0, 1 - r)):
+    for device in (at(-2), at(-2, 1 - r), at(-1), at(0, 1 - r)):
         pl.semaphore_signal(barrier, inc=1, device_id=device, device_id_type=MESH)
-    pl.semaphore_wait(barrier, 6)
-
-    def next_chip(g):
-        return remote(TO_NEXT_CHIP, g, qs.at[0, part(g)], qs.at[2, part(g)], at(2))
-
-    def next_block(g):
-        return remote(TO_NEXT, g, qs.at[2, part(g)], qs.at[3, part(g)], at(1))
-
-    def next_core(g):
-        return remote(TO_CORE, g, qs.at[2 * c, part(g)], qs.at[1, part(g)], partner)
+
+    @pl.when(c == 0)
+    def _():
+        pl.semaphore_signal(barrier, inc=1, device_id=partner, device_id_type=MESH)
+
+    loads[0].wait()
+    pl.semaphore_wait(barrier, 4 + c)
+    pl.semaphore_signal(ready.at[0], inc=1, device_id=at(1), device_id_type=MESH)
+    for rep in range(2):
+        pl.semaphore_signal(ready.at[1], inc=1, device_id=at(2, rep), device_id_type=MESH)
+
+    def next_chip(i):
+        return remote(TO_NEXT_CHIP, i, qs.at[0, chunk(i)], qs.at[2, chunk(i)], at(2))
+
+    def next_block(i):
+        return remote(TO_NEXT, i, qs.at[2, chunk(i)], qs.at[3, chunk(i)], at(1))
+
+    def next_core(i):
+        return remote(TO_CORE, i, qs.at[2 * c, chunk(i)], qs.at[1, chunk(i)], partner)
 
     def side(g):
         return (remote(SIDE, g, pf.at[1, :, part(g)], r1.at[:, part(g)], partner),
@@ -106,7 +123,7 @@
     scale = SHARPNESS / math.sqrt(depth)
 
     def attend(slot, g):
-        d = lax.dot_general(qs[slot, part(g)], ks[...], (((1,), (1,)), ((), ())), preferred_element_type=jnp.float32)
+        d = jnp.dot(qs[slot, part(g)], kt[...], preferred_element_type=jnp.float32)
         top = jnp.max(d, axis=1, keepdims=True)
         weights = jnp.exp2((d - top) * (scale * math.log2(math.e)))
         total = jnp.sum(weights, axis=1, keepdims=True)
@@ -116,16 +133,31 @@
             pf[slot, j, part(g)] = share * jnp.dot(low, vs[:, j * half:(j + 1) * half], preferred_element_type=jnp.float32)
         lp[slot, g] = as_tile(top * scale + jnp.log(total), rows)
 
-    loads[0].wait()
+    def chunks_of(g):
+        return range(g * each, (g + 1) * each)
 
     @pl.when(c == 0)
     def _():
-        for g in range(PARTS):
-            next_core(g).start()
-
-    for g in range(PARTS):
-        next_chip(g).start()
+        for i in range(CHUNKS):
+            next_core(i).start()
+
+    @pl.when(c == 1)
+    def _():
+        for i in range(CHUNKS):
+            next_chip(i).start()
+
+    @pl.when(jnp.logical_and(c == 0, place == 0))
+    def _():
+        for i in range(CHUNKS):
+            next_chip(i).start()
+
     loads[1].wait()
+
+    @pl.loop(0, ks.shape[0] // 256)
+    def _(i):
+        columns = pl.ds(pl.multiple_of(i * 256, 256), 256)
+        kt[:, columns] = ks[columns, :].T
+
     loads[2].wait()
     for g in range(PARTS):
         attend(0, g)
@@ -133,22 +165,35 @@
     for g in range(PARTS):
         @pl.when(c == 1)
         def _():
-            arrived(next_chip(g))
-            start(next_block(g), next_core(g))
-        arrived(next_core(g))
+            for i in chunks_of(g):
+                arrived(next_chip(i))
+                start(next_block(i), next_core(i))
+        for i in chunks_of(g):
+            arrived(next_core(i))
         attend(1, g)
         start(*side(g))
 
+        @pl.when(jnp.logical_and(c == 0, place == 1))
+        def _():
+            for i in chunks_of(g):
+                next_chip(i).start()
+
     def returned(g):
         p3[:, part(g)] = pf[3, :, part(g)].astype(jnp.bfloat16)
+        if g == 0:
+            pl.semaphore_wait(ready.at[0], 1)
         start(*back(g))
 
     for g in range(PARTS):
         @pl.when(c == 0)
         def _():
-            arrived(next_chip(g))
-            start(next_block(g))
-            arrived(next_block(g))
+            for i in chunks_of(g):
+                arrived(next_block(i))
+
+        @pl.when(jnp.logical_and(c == 0, place >= 2))
+        def _():
+            for i in chunks_of(g):
+                next_chip(i).start()
         attend(3 - c, g)
 
         @pl.when(c == 0)
@@ -166,15 +211,9 @@
         lo[g] = as_tile(both, rows)
         start(*across(g))
 
-    for g in range(PARTS):
-        @pl.when(c == 1)
-        def _():
-            arrived(next_block(g))
-        attend(2 + c, g)
-
-        @pl.when(c == 1)
-        def _():
-            returned(g)
+    def merge(g):
+        if g == 0:
+            pl.semaphore_wait(ready.at[1], 2)
         arrived(*back(g))
         mine = as_column(lp[2, g], rows)
         core = jnp.where(c == 1, as_column(l1[g], rows), NEVER)
@@ -186,6 +225,28 @@
             ms[j, part(g)] = (mine * pf[2, j, part(g)] + core * r1[j, part(g)]
                               + behind * r3[j, part(g)].astype(jnp.float32)).astype(jnp.bfloat16)
             start(*home(g, j, r))
+
+    for g in range(PARTS):
+        @pl.when(c == 0)
+        def _():
+            for i in chunks_of(g):
+                arrived(next_chip(i))
+                start(next_block(i))
+
+        @pl.when(c == 1)
+        def _():
+            merge(g)
+            for i in chunks_of(g):
+                arrived(next_block(i))
+        attend(2 + c, g)
+
+        @pl.when(c == 1)
+        def _():
+            returned(g)
+
+        @pl.when(c == 0)
+        def _():
+            merge(g)
 
     column = pl.ds(pl.multiple_of(r * half, half), half)
     outs = []
@@ -207,9 +268,19 @@
         out.wait()
     for g in range(PARTS):
         arrived(final(g, column))
-        for copy in (next_chip(g), next_block(g), next_core(g), *side(g), *back(g), *across(g),
+        for copy in (*side(g), *back(g), *across(g),
                      *home(g, 0, r), *home(g, 1, r), final(g, column)):
             copy.wait_send()
+    for i in range(CHUNKS):
+        for copy in (next_chip(i), next_block(i), next_core(i)):
+            copy.wait_send()
+
+
+def settle(attributed, log_total, out, log_out):
+    out[...] = attributed[...]
+    rows = log_total.shape[1]
+    for g in range(log_total.shape[0]):
+        log_out[pl.ds(g * rows, rows)] = log_total[g]
 
 
 def shards(n, queries, corpus, attributions):
@@ -226,6 +297,7 @@
         scratch_shapes=[
             pltpu.VMEM((4, block, depth), low),
             pltpu.VMEM((slab, depth), low),
+            pltpu.VMEM((depth, slab), low),
             pltpu.VMEM((slab, width), low),
             pltpu.VMEM((4, 2, block, half), full),
             pltpu.VMEM((2, block, half), full),
@@ -245,13 +317,19 @@
             pltpu.VMEM((PARTS, 8, rows), full),
             pltpu.VMEM((2, PARTS, 8, rows), full),
             pltpu.SemaphoreType.DMA((3,)),
-            pltpu.SemaphoreType.DMA((14, PARTS)),
-            pltpu.SemaphoreType.DMA((14, PARTS)),
+            pltpu.SemaphoreType.DMA((14, CHUNKS)),
+            pltpu.SemaphoreType.DMA((14, CHUNKS)),
             pltpu.SemaphoreType.DMA((PARTS,)),
+            pltpu.SemaphoreType.REGULAR((2,)),
         ],
         compiler_params=pltpu.CompilerParams(collective_id=0, has_side_effects=True, vmem_limit_bytes=60 << 20),
     )(queries, corpus, attributions)
-    return attributed, log_total.reshape(block)
+    return pl.pallas_call(
+        settle,
+        out_shape=(jax.ShapeDtypeStruct((block, width), low), jax.ShapeDtypeStruct((block,), full)),
+        in_specs=[pl.BlockSpec(memory_space=pltpu.VMEM)] * 2,
+        out_specs=(pl.BlockSpec(memory_space=pltpu.VMEM), pl.BlockSpec(memory_space=pltpu.VMEM)),
+    )(attributed, log_total)
 
 
 def solution(mesh):

time: 58.4 us -> 52.4 us (0.90)
  the two profiles are of different devices: /device:TPU:0 before, /device:TPU:234 now
where the time goes in v2:
time: 52.4 us; the launch traced here: 52.3 us
  Pallas kernels  51.7 us (99%)
  between operations  0.64 us (1%)
    pallas_call x1, Pallas kernels, shards(): pl.pallas_call(functools.partial(kernel, n), out_shape=(jax.ShapeDtypeStr...  49.8 us
    pallas_call x1, Pallas kernels, shards(): pl.pallas_call(settle, out_shape=(jax.ShapeDtypeStruct((block, width), lo...  1.87 us

profile of v2, /device:TPU:234, one launch (start us, length us, event | category | flops | bytes accessed | tf_op | source)
XLA Modules:
  0.0 52.3 jit_solution(3618590549981686144)
XLA Ops:
  0.6 49.8 %shard_map.50 = (bf16[256,1024]{1,0:T(8,128)(2,1)}, f32[2,128]{1,0:T(2,128)}) custom-call(bf16[256,1024]{1,0:T(8,128)(2,1)} %q_hbm.1, bf16[1,2048,1024]{2,1,0:T(8,128)(2,1)} %k_hbm.1, bf16[1,2048,1024]{2,1,0:T(8,128)(2,1)} %v_hbm.1), custom_call_target="tpu_custom_call" | custom-call | tf_op jit(solution)/shard_map/pallas_call | solution.py:292
  50.4 1.9 %shard_map.51 = (bf16[256,1024]{1,0:T(8,128)(2,1)}, f32[256]{0:T(256)}) custom-call(bf16[256,1024]{1,0:T(8,128)(2,1)} %get-tuple-element.4.attributed, f32[2,128]{1,0:T(2,128)} %get-tuple-element.5.log_total), custom_call_target="tpu_custom_call" | custom-call | tf_op jit(solution)/shard_map/pallas_call | solution.py:327

commit v3 on v2

--- a/solution.py
+++ b/solution.py
@@ -105,12 +105,14 @@
         return (remote(OWN, g, xs.at[part(g)], rx.at[part(g)], at(0, 1 - r)),
                 remote(OWN_L, g, lo.at[g], lx.at[g], at(0, 1 - r)))
 
-    def home(g, j, source):
-        return (remote(HOME + 2 * j, g, ms.at[j, part(g)], rm.at[source, part(g)], at(-2, j), HOME + 2 * source),
-                remote(HOME_L + 2 * j, g, lm.at[g], lr.at[source, g], at(-2, j), HOME_L + 2 * source))
-
-    def final(g, column):
-        return remote(FINAL, g, fin.at[part(g)], out_hbm.at[part(g), column], at(0, 1 - r))
+    def home(i, j, source):
+        return remote(HOME + 2 * j, i, ms.at[j, chunk(i)], rm.at[source, chunk(i)], at(-2, j), HOME + 2 * source)
+
+    def home_l(g, j, source):
+        return remote(HOME_L + 2 * j, g, lm.at[g], lr.at[source, g], at(-2, j), HOME_L + 2 * source)
+
+    def final(i, column):
+        return remote(FINAL, i, fin.at[chunk(i)], out_hbm.at[chunk(i), column], at(0, 1 - r))
 
     def start(*copies):
         for copy in copies:
@@ -146,21 +148,21 @@
         for i in range(CHUNKS):
             next_chip(i).start()
 
+    loads[1].wait()
+
+    @pl.loop(0, ks.shape[0] // 256)
+    def _(i):
+        columns = pl.ds(pl.multiple_of(i * 256, 256), 256)
+        kt[:, columns] = ks[columns, :].T
+
+    loads[2].wait()
+    for g in range(PARTS):
+        attend(0, g)
+
     @pl.when(jnp.logical_and(c == 0, place == 0))
     def _():
         for i in range(CHUNKS):
             next_chip(i).start()
-
-    loads[1].wait()
-
-    @pl.loop(0, ks.shape[0] // 256)
-    def _(i):
-        columns = pl.ds(pl.multiple_of(i * 256, 256), 256)
-        kt[:, columns] = ks[columns, :].T
-
-    loads[2].wait()
-    for g in range(PARTS):
-        attend(0, g)
 
     for g in range(PARTS):
         @pl.when(c == 1)
@@ -221,10 +223,14 @@
         both = log_sum([mine, core, behind])
         mine, core, behind = jnp.exp(mine - both), jnp.exp(core - both), jnp.exp(behind - both)
         lm[g] = as_tile(both, rows)
-        for j in range(2):
-            ms[j, part(g)] = (mine * pf[2, j, part(g)] + core * r1[j, part(g)]
-                              + behind * r3[j, part(g)].astype(jnp.float32)).astype(jnp.bfloat16)
-            start(*home(g, j, r))
+        for j in (1 - r, r):
+            start(home_l(g, j, r))
+        for i in chunks_of(g):
+            these = slice((i - g * each) * few, (i - g * each + 1) * few)
+            for j in (1 - r, r):
+                ms[j, chunk(i)] = (mine[these] * pf[2, j, chunk(i)] + core[these] * r1[j, chunk(i)]
+                                   + behind[these] * r3[j, chunk(i)].astype(jnp.float32)).astype(jnp.bfloat16)
+                start(home(i, j, r))
 
     for g in range(PARTS):
         @pl.when(c == 0)
@@ -251,25 +257,30 @@
     column = pl.ds(pl.multiple_of(r * half, half), half)
     outs = []
     for g in range(PARTS):
-        arrived(*across(g), *home(g, 0, 0), *home(g, 1, 1))
+        arrived(*across(g), home_l(g, 0, 0), home_l(g, 1, 1))
         logs = [as_column(t, rows) for t in (lo[g], lx[g], lr[0, g], lr[1, g])]
         both = log_sum(logs)
         w = [jnp.exp(t - both) for t in logs]
-        fin[part(g)] = (w[0] * own[part(g)] + w[1] * rx[part(g)].astype(jnp.float32)
-                        + w[2] * rm[0, part(g)].astype(jnp.float32)
-                        + w[3] * rm[1, part(g)].astype(jnp.float32)).astype(jnp.bfloat16)
-        final(g, column).start()
-        out = pltpu.make_async_copy(fin.at[part(g)], out_hbm.at[part(g), column], out_sem.at[g])
-        out.start()
-        outs.append(out)
         log_ref[g:g + 1] = as_tile(both, rows)[0:1]
+        for i in chunks_of(g):
+            these = slice((i - g * each) * few, (i - g * each + 1) * few)
+            arrived(home(i, 0, 0), home(i, 1, 1))
+            fin[chunk(i)] = (w[0][these] * own[chunk(i)] + w[1][these] * rx[chunk(i)].astype(jnp.float32)
+                             + w[2][these] * rm[0, chunk(i)].astype(jnp.float32)
+                             + w[3][these] * rm[1, chunk(i)].astype(jnp.float32)).astype(jnp.bfloat16)
+            final(i, column).start()
+            out = pltpu.make_async_copy(fin.at[chunk(i)], out_hbm.at[chunk(i), column], out_sem.at[i])
+            out.start()
+            outs.append(out)
 
     for out in outs:
         out.wait()
     for g in range(PARTS):
-        arrived(final(g, column))
-        for copy in (*side(g), *back(g), *across(g),
-                     *home(g, 0, r), *home(g, 1, r), final(g, column)):
+        for copy in (*side(g), *back(g), *across(g), home_l(g, 0, r), home_l(g, 1, r)):
+            copy.wait_send()
+    for i in range(CHUNKS):
+        arrived(final(i, column))
+        for copy in (home(i, 0, r), home(i, 1, r), final(i, column)):
             copy.wait_send()
     for i in range(CHUNKS):
         for copy in (next_chip(i), next_block(i), next_core(i)):
@@ -319,7 +330,7 @@
             pltpu.SemaphoreType.DMA((3,)),
             pltpu.SemaphoreType.DMA((14, CHUNKS)),
             pltpu.SemaphoreType.DMA((14, CHUNKS)),
-            pltpu.SemaphoreType.DMA((PARTS,)),
+            pltpu.SemaphoreType.DMA((CHUNKS,)),
             pltpu.SemaphoreType.REGULAR((2,)),
         ],
         compiler_params=pltpu.CompilerParams(collective_id=0, has_side_effects=True, vmem_limit_bytes=60 << 20),

time: 52.4 us -> 49.7 us (0.948)
  the two profiles are of different devices: /device:TPU:234 before, /device:TPU:0 now
where the time goes in v3:
time: 49.7 us; the launch traced here: 48.8 us
  Pallas kernels  48.1 us (97%)
  between operations  0.64 us (1%)
    pallas_call x1, Pallas kernels, shards(): pl.pallas_call(functools.partial(kernel, n), out_shape=(jax.ShapeDtypeStr...  46.3 us
    pallas_call x1, Pallas kernels, shards(): pl.pallas_call(settle, out_shape=(jax.ShapeDtypeStruct((block, width), lo...  1.87 us

profile of v3, /device:TPU:0, one launch (start us, length us, event | category | flops | bytes accessed | tf_op | source)
XLA Modules:
  0.0 48.8 jit_solution(10046740622603567751)
XLA Ops:
  0.6 46.3 %shard_map.50 = (bf16[256,1024]{1,0:T(8,128)(2,1)}, f32[2,128]{1,0:T(2,128)}) custom-call(bf16[256,1024]{1,0:T(8,128)(2,1)} %q_hbm.1, bf16[1,2048,1024]{2,1,0:T(8,128)(2,1)} %k_hbm.1, bf16[1,2048,1024]{2,1,0:T(8,128)(2,1)} %v_hbm.1), custom_call_target="tpu_custom_call" | custom-call | tf_op jit(solution)/shard_map/pallas_call | solution.py:303
  46.9 1.9 %shard_map.51 = (bf16[256,1024]{1,0:T(8,128)(2,1)}, f32[256]{0:T(256)}) custom-call(bf16[256,1024]{1,0:T(8,128)(2,1)} %get-tuple-element.4.attributed, f32[2,128]{1,0:T(2,128)} %get-tuple-element.5.log_total), custom_call_target="tpu_custom_call" | custom-call | tf_op jit(solution)/shard_map/pallas_call | solution.py:338
